TPU v7x, 32 devices: a whole 2x2x4 slice. The times are simulated.
32 devices in a mesh: vec: 16 (over z, y, x), ao: 2 (over core).
Axes of the slice: x: 2, y: 2, z: 4, core: 2. Of those that a mesh axis runs over, the one named last changes fastest.
Arguments:
- cholesky: float32 [16, 1200, 1200], P('vec', 'ao'), may hold values from -6 to 6
- coefficients: float32 [2, 720000], P('ao', 'vec'), may hold values from -0.1875 to 0.1875
Outputs:
- mo_vectors: float32 [16, 128, 1072], P(None, 'vec', 'ao')
All inputs are finite; a program needn't handle non-finite values.
Results may differ from a plain program's by a relative error of at most 0.0001.
Values sent between devices are 32-bit elements; how exact they have to be, the bound alone decides.
A program may use at most 64 MiB of HBM per device.

v0:
```python
import jax
import jax.numpy as jnp
from jax import lax
from jax.sharding import PartitionSpec as P

NOCC = 128


def body(cholesky, coefficients):
    half_rows = cholesky.shape[1]
    own_flat = lax.all_gather(coefficients, "vec", axis=1, tiled=True)
    own_rows = own_flat.reshape(half_rows, own_flat.shape[1] // half_rows)
    occupied_own = own_rows[:, :NOCC]
    partial_x = jnp.einsum(
        "mi,pmn->pin",
        occupied_own,
        cholesky,
        precision=lax.Precision.HIGHEST,
        preferred_element_type=jnp.float32,
    )
    x_block = lax.psum_scatter(partial_x, "ao", scatter_dimension=2, tiled=True)
    virtual_own = own_rows[:, NOCC:]
    partial_y = jnp.einsum(
        "pin,na->pia",
        x_block,
        virtual_own,
        precision=lax.Precision.HIGHEST,
        preferred_element_type=jnp.float32,
    )
    summed = lax.psum_scatter(partial_y, "ao", scatter_dimension=2, tiled=True)
    owned = lax.all_to_all(summed, "vec", split_axis=1, concat_axis=0, tiled=True)
    return owned


def solution(mesh):
    in_specs = (P("vec", "ao", None), P("ao", "vec"))
    out_specs = P(None, "vec", "ao")
    return jax.shard_map(body, mesh=mesh, in_specs=in_specs, out_specs=out_specs, check_vma=False)
```

profile of v0, /device:TPU:0, one launch (start us, length us, event | category | flops | bytes accessed | tf_op | source)
XLA Modules:
  0.0 220.5 jit_solution(14244997338164089327)
XLA Ops:
  6.5 0.0 copy-start
  6.5 0.0 all-reduce.5.cloned.1.call-start
  6.5 1.4 dynamic-slice
  8.6 1.8 broadcast
  10.3 2.5 %dynamic-update-slice = f32[720000]{0:T(1024)} dynamic-update-slice(f32[720000]{0:T(1024)} %broadcast, f32[45000]{0:T(1024)} %bitcast.30, u32[]{:T(128)} %bitcast.1) | dynamic-update-slice | bytes 360004
  12.9 0.0 all-reduce.5.cloned.1.call-update
  12.9 0.0 reduce-scatter.11.cloned.1.call-start
  13.0 144.7 %all-reduce.5.cloned.1.call-done = f32[720000]{0:T(1024)} async-done(((f32[720000]{0:T(1024)}), f32[720000]{0:T(1024)}) %all-reduce.5.cloned.1.call-update) | async-done | bytes 2880016
  157.6 4.8 %reshape.15 = f32[600,1200]{1,0:T(8,128)} reshape(f32[720000]{0:T(1024)} %all-reduce.5.cloned.1.call-done) | data formatting | bytes 5760000 | tf_op jit(solution)/shard_map/reshape | solution.py:12
  162.4 0.0 copy-done
  162.4 7.1 %fusion.7 = f32[1,128,1200]{1,2,0:T(8,128)} fusion(f32[1,600,1200]{2,1,0:T(8,128)S(1)} %copy-done, f32[600,1200]{1,0:T(8,128)} %reshape.15), kind=kOutput, calls=%fused_computation.5 | convolution fusion | flops 1105920000 | bytes 3801600 | tf_op jit(solution)/shard_map/mi,pmn->pin/dot_general | solution.py:14
  169.5 0.0 reduce-scatter.11.cloned.1.call-update
  169.5 0.0 reduce-scatter.13.cloned.1.call-start
  169.6 7.4 %reduce-scatter.11.cloned.1.call-done = f32[1,128,600]{1,2,0:T(8,128)} async-done(((f32[1,128,1200]{1,2,0:T(8,128)}), f32[1,128,600]{1,2,0:T(8,128)}) %reduce-scatter.11.cloned.1.call-update) | async-done | bytes 307216
  176.9 7.4 %fusion.4 = f32[1,128,1072]{1,2,0:T(8,128)} fusion(f32[600,1200]{1,0:T(8,128)} %reshape.15, f32[1,128,600]{1,2,0:T(8,128)} %reduce-scatter.11.cloned.1.call-done), kind=kOutput, calls=%fused_computation.4 | convolution fusion | flops 987955200 | bytes 3620864 | tf_op jit(solution)/shard_map/pin,na->pia/dot_general | solution.py:23
  184.4 0.0 reduce-scatter.13.cloned.1.call-update
  184.4 9.2 %reduce-scatter.13.cloned.1.call-done = f32[1,128,536]{1,2,0:T(8,128)} async-done(((f32[1,128,1072]{1,2,0:T(8,128)}), f32[1,128,536]{1,2,0:T(8,128)}) %reduce-scatter.13.cloned.1.call-update) | async-done | bytes 274448
  193.6 1.1 copy.5
  194.8 18.4 %all_to_all.12 = f32[1,128,536]{2,0,1:T(1,128)S(1)} all-to-all(f32[1,128,536]{2,0,1:T(1,128)S(1)} %copy.5), channel_id=1, replica_groups=mesh['vec'=16,'ao'=2] {'vec'}, dimensions={1} | all-to-all | bytes 548864 | tf_op jit(solution)/shard_map/all_to_all | solution.py:31
  213.2 0.7 copy.12
Async XLA Ops:
  6.5 155.9 %copy-start = (f32[1,600,1200]{2,1,0:T(8,128)S(1)}, f32[1,600,1200]{2,1,0:T(8,128)}, u32[]{:S(2)}) copy-start(f32[1,600,1200]{2,1,0:T(8,128)} %param.2) | copy-start | bytes 8640004
  6.5 151.1 %all-reduce.5.cloned.1.call-start = ((), (), s32[]{:S(2)}) async-start(), calls=%async_computation.3 | async-start | bytes 5767168
  12.9 164.0 %reduce-scatter.11.cloned.1.call-start = ((), (), s32[]{:S(2)}) async-start(), calls=%async_computation.4 | async-start | bytes 921600
  169.5 24.1 %reduce-scatter.13.cloned.1.call-start = ((), (), s32[]{:S(2)}) async-start(), calls=%async_computation.5 | async-start | bytes 823296
Sparse Core Ops, SparseCore 0:
  13.0 144.5 all-reduce.4
  169.7 7.2 reduce-scatter.10
  184.5 9.0 reduce-scatter.12
where the time goes:
time: 221 us; the launch traced here: 220 us
  waiting for transfers between devices  161 us (73%)
  blocking collectives  18.4 us (8%)
  matrix products  14.5 us (7%)
  between operations  13.8 us (6%)
  local copies, waits for them, and re-layouts  12.4 us (6%)
    unnamed x6, waiting for transfers between devices  161 us
    all_to_all x1, blocking collectives, body(): lax.all_to_all(summed, 'vec', split_axis=1, concat_axis=0, tiled=True)  18.4 us
    dot_general x1, matrix products, body(): jnp.einsum('pin,na->pia', x_block, virtual_own, precision=lax.Precision.H...  7.43 us
    dot_general x1, matrix products, body(): jnp.einsum('mi,pmn->pin', occupied_own, cholesky, precision=lax.Precision...  7.07 us
    unnamed x6, local copies, waits for them, and re-layouts  6.45 us
    reshape x1, local copies, waits for them, and re-layouts, body(): own_rows = own_flat.reshape(half_rows, own_flat.shape[1] // half_rows)  4.81 us
  transfers between devices with their start and end apart: 3, of which 3 were waited for; matrix products, arithmetic and copies ran while one was open for 0% of the time, Pallas kernels for 0%

commit v1 on v0

--- a/solution.py
+++ b/solution.py
@@ -1,12 +1,23 @@
+import functools
+
 import jax
 import jax.numpy as jnp
 from jax import lax
+from jax.experimental import pallas as pl
+from jax.experimental.pallas import tpu as pltpu
 from jax.sharding import PartitionSpec as P
 
 NOCC = 128
-
-
-def body(cholesky, coefficients):
+LANES = 128
+MESH = pl.DeviceIdType.MESH
+F32 = jnp.float32
+
+
+def up_to(size, step):
+    return -(-size // step) * step
+
+
+def simple_body(cholesky, coefficients):
     half_rows = cholesky.shape[1]
     own_flat = lax.all_gather(coefficients, "vec", axis=1, tiled=True)
     own_rows = own_flat.reshape(half_rows, own_flat.shape[1] // half_rows)
@@ -32,7 +43,222 @@
     return owned
 
 
+def split(value):
+    high = value.astype(jnp.bfloat16)
+    return high, (value - high.astype(F32)).astype(jnp.bfloat16)
+
+
+def product(left, right):
+    (lh, ll), (rh, rl) = left, right
+    dot = functools.partial(jnp.dot, preferred_element_type=F32)
+    return dot(lh, rh) + (dot(lh, rl) + dot(ll, rh))
+
+
+def kernel(
+    n, starts, rows, occ_ref, vir_ref, l_ref, out_ref,
+    occ_all, vir_all, l_buf, occ_dense, vir_dense, x_full, x_out, x_in, x_send, x_recv, y_full, y_out, y_in,
+    l_sem, occ_ss, occ_rs, vir_ss, vir_rs, x_ss, x_rs, pair_ss, pair_rs,
+):
+    me, core = lax.axis_index("vec"), lax.axis_index("ao")
+    nz = n // 4
+    x, y, z = me % 2, (me // 2) % 2, me // 4
+    xp, yp = me + 1 - 2 * x, me + 2 - 4 * y
+    half = l_ref.shape[0]
+    nao = l_ref.shape[1]
+
+    l_copy = pltpu.make_async_copy(l_ref, l_buf, l_sem)
+    l_copy.start()
+
+    barrier = pltpu.get_barrier_semaphore()
+    for d in range(1, n):
+        pl.semaphore_signal(barrier, inc=1, device_id=((me + d) % n, core), device_id_type=MESH)
+    pl.semaphore_signal(barrier, inc=1, device_id=(me, 1 - core), device_id_type=MESH)
+    pl.semaphore_wait(barrier, n)
+
+    def occ_copy(w, to):
+        return pltpu.make_async_remote_copy(
+            src_ref=occ_ref, dst_ref=occ_all.at[w], send_sem=occ_ss.at[to], recv_sem=occ_rs.at[w],
+            device_id=(to, core), device_id_type=MESH)
+
+    def vir_copy(w, way, to, src=None):
+        return pltpu.make_async_remote_copy(
+            src_ref=vir_all.at[w] if src is None else src, dst_ref=vir_all.at[w],
+            send_sem=vir_ss.at[way, w], recv_sem=vir_rs.at[w], device_id=(to, core), device_id_type=MESH)
+
+    def x_copy(w, to):
+        return pltpu.make_async_remote_copy(
+            src_ref=x_send.at[to], dst_ref=x_recv.at[w], send_sem=x_ss.at[to], recv_sem=x_rs.at[w],
+            device_id=(to, core), device_id_type=MESH)
+
+    def pair_copy(which, src, dst):
+        return pltpu.make_async_remote_copy(
+            src_ref=src, dst_ref=dst, send_sem=pair_ss.at[which], recv_sem=pair_rs.at[which],
+            device_id=(me, 1 - core), device_id_type=MESH)
+
+    for d in range(1, n):
+        occ_copy(me, (me + d) % n).start()
+    pl.when(z < nz - 1)(lambda: vir_copy(me, 2, me + 4, vir_ref).start())
+    pl.when(z > 0)(lambda: vir_copy(me, 3, me - 4, vir_ref).start())
+    vir_copy(me, 0, xp, vir_ref).start()
+    vir_copy(me, 1, yp, vir_ref).start()
+
+    def line(k):
+        @pl.when(z >= k)
+        def _():
+            w = me - 4 * k
+            vir_copy(w, 2, me).wait_recv()
+            pl.when(z < nz - 1)(lambda: vir_copy(w, 2, me + 4).start())
+            vir_copy(w, 0, xp).start()
+            vir_copy(w, 1, yp).start()
+
+        @pl.when(z + k < nz)
+        def _():
+            w = me + 4 * k
+            vir_copy(w, 3, me).wait_recv()
+            pl.when(z > 0)(lambda: vir_copy(w, 3, me - 4).start())
+            vir_copy(w, 0, xp).start()
+            vir_copy(w, 1, yp).start()
+
+    def plane(k):
+        def one(zz, shift):
+            wx, wy = xp + 4 * shift, yp + 4 * shift
+            vir_copy(wx, 0, me).wait_recv()
+            pl.when(zz % 2 == 0)(lambda: vir_copy(wx, 1, yp).start())
+            vir_copy(wy, 1, me).wait_recv()
+            pl.when(zz % 2 == 1)(lambda: vir_copy(wy, 0, xp).start())
+
+        if k == 0:
+            one(z, 0)
+        else:
+            pl.when(z >= k)(lambda: one(z - k, -k))
+            pl.when(z + k < nz)(lambda: one(z + k, k))
+
+    occ_all[me] = occ_ref[...]
+    vir_all[me] = vir_ref[...]
+    occ_dense[...] = jnp.zeros_like(occ_dense)
+    vir_dense[...] = jnp.zeros_like(vir_dense)
+    x_full[...] = jnp.zeros_like(x_full)
+    line(1)
+    for d in range(1, n):
+        occ_copy((me + d) % n, me).wait_recv()
+    for w in range(n):
+        occ_dense[starts[w]:starts[w] + rows, :] += occ_all[w, :rows, :]
+    l_copy.wait()
+    occ_t = occ_dense[...].T[:, :half]
+    x_full[:, :nao] = product(split(occ_t), split(l_buf[...]))
+    whole = x_full[...]
+    low = whole[:, :x_out.shape[1]]
+    high = pltpu.roll(whole, x_full.shape[1] - half, 1)[:, :x_out.shape[1]]
+    first = core == 0
+    x_out[...] = jnp.where(first, high, low)
+    x_own = jnp.where(first, low, high)
+    pair_copy(0, x_out, x_in).start()
+    plane(0)
+    if nz > 2:
+        line(2)
+    pair_copy(0, x_out, x_in).wait_recv()
+    x_sum = x_own + x_in[...]
+    x_send[...] = x_sum.reshape(x_send.shape)
+    if nz > 1:
+        plane(1)
+    for d in range(1, n):
+        x_copy(me, (me + d) % n).start()
+    x_recv[me] = x_send[me]
+    for k in range(2, nz):
+        if k + 1 < nz:
+            line(k + 1)
+        plane(k)
+    for zz in range(nz):
+        wd = (1 - x) + 2 * (1 - y) + 4 * zz
+        vir_copy(wd, 0, me).wait_recv()
+    for d in range(1, n):
+        x_copy((me + d) % n, me).wait_recv()
+    for w in range(n):
+        vir_dense[starts[w]:starts[w] + rows, :] += vir_all[w, :rows, :]
+    y_full[...] = product(split(x_recv[...].reshape(x_sum.shape)), split(vir_dense[...]))
+    whole_y = y_full[...]
+    low_y = whole_y[:, :y_out.shape[1]]
+    high_y = pltpu.roll(whole_y, y_full.shape[1] - out_ref.shape[2], 1)[:, :y_out.shape[1]]
+    y_out[...] = jnp.where(first, high_y, low_y)
+    y_own = jnp.where(first, low_y, high_y)
+    pair_copy(1, y_out, y_in).start()
+
+    for d in range(1, n):
+        occ_copy(me, (me + d) % n).wait_send()
+        x_copy(me, (me + d) % n).wait_send()
+    for zz in range(nz):
+        w = x + 2 * y + 4 * zz
+        vir_copy(w, 0, xp).wait_send()
+        vir_copy(w, 1, yp).wait_send()
+        pl.when((z >= zz) & (z < nz - 1))(lambda w=w: vir_copy(w, 2, xp).wait_send())
+        pl.when((z <= zz) & (z > 0))(lambda w=w: vir_copy(w, 3, xp).wait_send())
+        if zz % 2 == 0:
+            vir_copy(xp + 4 * (zz - z), 1, yp).wait_send()
+        else:
+            vir_copy(yp + 4 * (zz - z), 0, xp).wait_send()
+    pair_copy(0, x_out, x_in).wait_send()
+    pair_copy(1, y_out, y_in).wait()
+    out_ref[...] = (y_own + y_in[...])[:, :out_ref.shape[2]].reshape(out_ref.shape)
+
+
+def body(n, cholesky, coefficients):
+    if cholesky.shape[0] != 1:
+        return simple_body(cholesky, coefficients)
+    half, nao = cholesky.shape[1:]
+    per = coefficients.shape[1]
+    nmo = per * n // half
+    nvir = nmo - NOCC
+    offsets = [w * per % nmo for w in range(n)]
+    starts = tuple(w * per // nmo for w in range(n))
+    rows = max(-(-(offset + per) // nmo) for offset in offsets)
+    deep = up_to(rows, 8)
+    me = lax.axis_index("vec")
+    flat = coefficients[0]
+    total = deep * nmo
+    framed = jnp.zeros((total,), F32)
+    for offset in sorted(set(offsets)):
+        here = jnp.pad(flat, (offset, total - per - offset))
+        framed = jnp.where(me * per % nmo == offset, here, framed)
+    framed = framed.reshape(deep, nmo)
+    occ = framed[:, :NOCC]
+    wide = up_to(nvir, LANES)
+    vir = jnp.pad(framed[:, NOCC:], ((0, 0), (0, wide - nvir)))
+    tall = up_to(max(half, starts[-1] + rows), LANES)
+    part = up_to(nvir // 2, LANES)
+    iblock = NOCC // n
+    dma = pltpu.SemaphoreType.DMA
+    vmem = pl.BlockSpec(memory_space=pltpu.VMEM)
+    return pl.pallas_call(
+        functools.partial(kernel, n, starts, rows),
+        out_shape=jax.ShapeDtypeStruct((n, iblock, nvir // 2), F32),
+        in_specs=[vmem, vmem, pl.BlockSpec(memory_space=pl.ANY)],
+        out_specs=vmem,
+        scratch_shapes=[
+            pltpu.VMEM((n, deep, NOCC), F32),
+            pltpu.VMEM((n, deep, wide), F32),
+            pltpu.VMEM((half, nao), F32),
+            pltpu.VMEM((tall, NOCC), F32),
+            pltpu.VMEM((tall, wide), F32),
+            pltpu.VMEM((NOCC, up_to(nao, LANES)), F32),
+            pltpu.VMEM((NOCC, tall), F32),
+            pltpu.VMEM((NOCC, tall), F32),
+            pltpu.VMEM((n, iblock, tall), F32),
+            pltpu.VMEM((n, iblock, tall), F32),
+            pltpu.VMEM((NOCC, wide), F32),
+            pltpu.VMEM((NOCC, part), F32),
+            pltpu.VMEM((NOCC, part), F32),
+            dma, dma((n,)), dma((n,)), dma((4, n)), dma((n,)), dma((n,)), dma((n,)), dma((2,)), dma((2,)),
+        ],
+        compiler_params=pltpu.CompilerParams(
+            collective_id=0, has_side_effects=True, vmem_limit_bytes=60 * 1024 * 1024),
+        name="transform",
+    )(occ, vir, cholesky[0])
+
+
 def solution(mesh):
+    n = mesh.shape["vec"]
     in_specs = (P("vec", "ao", None), P("ao", "vec"))
     out_specs = P(None, "vec", "ao")
-    return jax.shard_map(body, mesh=mesh, in_specs=in_specs, out_specs=out_specs, check_vma=False)
+    lines = n % 4 == 0 and mesh.shape["ao"] == 2 and NOCC % (8 * n) == 0
+    step = functools.partial(body, n) if lines else simple_body
+    return jax.shard_map(step, mesh=mesh, in_specs=in_specs, out_specs=out_specs, check_vma=False)

time: 221 us -> 56.7 us (0.26)
  waiting for transfers between devices: 161 us -> 0 us
  Pallas kernels: 0 us -> 52.2 us
  blocking collectives: 18.4 us -> 0 us
  matrix products: 14.5 us -> 0 us
  between operations: 13.8 us -> 0.03 us
  local copies, waits for them, and re-layouts: 12.4 us -> 3.2 us
    unnamed x6 -> x0, waiting for transfers between devices: 161 us -> none
    pallas_call x0 -> x1, Pallas kernels: none -> 52.2 us  [body(): pl.pallas_call(functools.partial(kernel, n, starts, rows), out_shape=jax....]
    all_to_all x1 -> x0, blocking collectives: 18.4 us -> none  [body(): lax.all_to_all(summed, 'vec', split_axis=1, concat_axis=0, tiled=True)]
    dot_general x2 -> x0, matrix products: 14.5 us -> none  [the longest x1 7.43 us: body(): jnp.einsum('pin,na->pia', x_block, virtual_own, precision=lax.Precision.H...]
    unnamed x6 -> x1, local copies, waits for them, and re-layouts: 6.45 us -> 1.72 us
    reshape x1, local copies, waits for them, and re-layouts: 4.81 us -> 0.16 us  [body(): framed = framed.reshape(deep, nmo)]
  transfers between devices with their start and end apart: 3 -> 0, of which waited for: 3 -> 0; matrix products, arithmetic and copies ran while one was open for 0% -> 0% of each run, Pallas kernels for 0% -> 0%
where the time goes in v1:
time: 56.7 us; the launch traced here: 56.5 us
  Pallas kernels  52.2 us (92%)
  local copies, waits for them, and re-layouts  3.2 us (6%)
  other arithmetic  1.12 us (2%)
    pallas_call x1, Pallas kernels, body(): pl.pallas_call(functools.partial(kernel, n, starts, rows), out_shape=jax....  52.2 us
    unnamed x1, local copies, waits for them, and re-layouts  1.72 us

profile of v1, /device:TPU:0, one launch (start us, length us, event | category | flops | bytes accessed | tf_op | source)
XLA Modules:
  0.0 56.5 jit_solution(6837888607957350817)
XLA Ops:
  0.0 1.1 %select_select_fusion = f32[48000]{0:T(1024)S(1)} fusion(f32[45000]{0:T(1024)} %bitcast.3, pred[]{:T(512)S(6)} %eq.10, pred[]{:T(512)S(6)} %eq.9), kind=kLoop, calls=%fused_computation | loop fusion | flops 96000 | bytes 372002 | tf_op jit(solution)/shard_map/jit(_where)/select_n | solution.py:221
  1.1 0.2 reshape.3
  1.3 0.6 %slice.8.occ_ref = f32[40,128]{1,0:T(8,128)} slice(f32[40,1200]{1,0:T(8,128)S(1)} %reshape.3), slice={[0:40], [0:128]} | slice | bytes 40960 | tf_op jit(solution)/shard_map/slice | solution.py:223
  1.9 0.7 %pad.14.vir_ref = f32[40,1152]{1,0:T(8,128)} pad(f32[40,1072]{1,0:T(8,128)S(1)} %slice.9, f32[]{:T(128)} %constant.25.clone.1), padding=0_0x0_80 | pad | bytes 355844 | tf_op jit(solution)/shard_map/jit(_pad)/pad | solution.py:225
  2.6 52.2 %transform.1 = f32[16,8,536]{2,1,0:T(8,128)} custom-call(f32[40,128]{1,0:T(8,128)} %slice.8.occ_ref, f32[40,1152]{1,0:T(8,128)} %pad.14.vir_ref, f32[600,1200]{1,0:T(8,128)} %bitcast.2), custom_call_target="tpu_custom_call" | custom-call | tf_op jit(solution)/shard_map/transform/pallas_call | solution.py:231
  54.8 1.7 %copy.4 = f32[16,8,536]{2,1,0:T(8,128)} copy(f32[16,8,536]{2,1,0:T(8,128)} %transform.1) | data formatting | bytes 548864
  (1 shorter events, 0.0 us)

commit v2 on v1

v2 whole, which is shorter than its diff:
```python
import functools

import jax
import jax.numpy as jnp
from jax import lax
from jax.experimental import pallas as pl
from jax.experimental.pallas import tpu as pltpu
from jax.sharding import PartitionSpec as P

NOCC = 128
LANES = 128
MESH = pl.DeviceIdType.MESH
F32 = jnp.float32
STEP, TURN = 16, 0


def up_to(size, step):
    return -(-size // step) * step


def simple_body(cholesky, coefficients):
    half_rows = cholesky.shape[1]
    own_flat = lax.all_gather(coefficients, "vec", axis=1, tiled=True)
    own_rows = own_flat.reshape(half_rows, own_flat.shape[1] // half_rows)
    occupied_own = own_rows[:, :NOCC]
    partial_x = jnp.einsum(
        "mi,pmn->pin",
        occupied_own,
        cholesky,
        precision=lax.Precision.HIGHEST,
        preferred_element_type=jnp.float32,
    )
    x_block = lax.psum_scatter(partial_x, "ao", scatter_dimension=2, tiled=True)
    virtual_own = own_rows[:, NOCC:]
    partial_y = jnp.einsum(
        "pin,na->pia",
        x_block,
        virtual_own,
        precision=lax.Precision.HIGHEST,
        preferred_element_type=jnp.float32,
    )
    summed = lax.psum_scatter(partial_y, "ao", scatter_dimension=2, tiled=True)
    owned = lax.all_to_all(summed, "vec", split_axis=1, concat_axis=0, tiled=True)
    return owned


def split(value):
    high = value.astype(jnp.bfloat16)
    return high, (value - high.astype(F32)).astype(jnp.bfloat16)


def product(left, right):
    (lh, ll), (rh, rl) = left, right
    dot = functools.partial(jnp.dot, preferred_element_type=F32)
    return dot(lh, rh) + (dot(lh, rl) + dot(ll, rh))


def kernel(
    n, starts, rows, pieces, plan, own_ref, l_ref, out_ref,
    rows_all, l_buf, occ_dense, vir_dense, x_full, x_out, x_in, x_send, x_recv, y_full, y_out, y_in,
    l_sem, occ_ss, occ_rs, vir_ss, vir_rs, x_ss, x_rs, pair_ss, pair_rs,
):
    me, core = lax.axis_index("vec"), lax.axis_index("ao")
    nz = n // 4
    x, y, z = me % 2, (me // 2) % 2, me // 4
    xp, yp, diag = me + 1 - 2 * x, me + 2 - 4 * y, me + 3 - 2 * x - 4 * y
    half, nao = l_ref.shape
    wide = vir_dense.shape[1]

    l_copy = pltpu.make_async_copy(l_ref, l_buf, l_sem)
    l_copy.start()
    rows_all[me, :, :own_ref.shape[1]] = own_ref[...]

    barrier = pltpu.get_barrier_semaphore()
    for d in range(1, n):
        pl.semaphore_signal(barrier, inc=1, device_id=((me + d) % n, core), device_id_type=MESH)
    pl.semaphore_signal(barrier, inc=1, device_id=(me, 1 - core), device_id_type=MESH)
    pl.semaphore_wait(barrier, n)

    def occ_copy(w, to):
        part = rows_all.at[w, :, pl.ds(0, NOCC)]
        return pltpu.make_async_remote_copy(
            src_ref=part, dst_ref=part, send_sem=occ_ss.at[to], recv_sem=occ_rs.at[w],
            device_id=(to, core), device_id_type=MESH)

    def vir_copy(p, w, way, to):
        part = rows_all.at[w, pl.ds(pieces[p][0], pieces[p][1]), pl.ds(NOCC, wide)]
        return pltpu.make_async_remote_copy(
            src_ref=part, dst_ref=part, send_sem=vir_ss.at[p, way, w], recv_sem=vir_rs.at[p, w],
            device_id=(to, core), device_id_type=MESH)

    def x_copy(w, to):
        return pltpu.make_async_remote_copy(
            src_ref=x_send.at[to], dst_ref=x_recv.at[w], send_sem=x_ss.at[to], recv_sem=x_rs.at[w],
            device_id=(to, core), device_id_type=MESH)

    def pair_copy(which, src, dst):
        return pltpu.make_async_remote_copy(
            src_ref=src, dst_ref=dst, send_sem=pair_ss.at[which], recv_sem=pair_rs.at[which],
            device_id=(me, 1 - core), device_id_type=MESH)

    def along(p, w, up=True, down=True):
        if up:
            pl.when(z < nz - 1)(lambda: vir_copy(p, w, 2, me + 4).start())
        if down:
            pl.when(z > 0)(lambda: vir_copy(p, w, 3, me - 4).start())

    def send_own(p):
        along(p, me)
        vir_copy(p, me, 0, xp).start()
        vir_copy(p, me, 1, yp).start()

    def line(k, p):
        if k >= nz:
            return
        for up in (True, False):
            @pl.when(z >= k if up else z + k < nz)
            def _():
                w = me - 4 * k if up else me + 4 * k
                vir_copy(p, w, 2, me).wait_recv()
                along(p, w, up, not up)
                vir_copy(p, w, 0, xp).start()
                vir_copy(p, w, 1, yp).start()

    def plane(k, p):
        def one(shift):
            wx, wy = xp + 4 * shift, yp + 4 * shift
            even = (z + shift) % 2 == 0
            cross = k == 0 or not pieces[p][2]
            vir_copy(p, wx, 0, me).wait_recv()
            if cross:
                pl.when(even)(lambda: vir_copy(p, wx, 1, yp).start())
            vir_copy(p, wy, 1, me).wait_recv()
            if cross:
                pl.when(jnp.logical_not(even))(lambda: vir_copy(p, wy, 0, xp).start())

        if k == 0:
            one(0)
        elif k < nz:
            pl.when(z >= k)(lambda: one(-k))
            pl.when(z + k < nz)(lambda: one(k))

    def corner(k, p):
        def one(shift, up, down):
            vir_copy(p, diag + 4 * shift, 0, me).wait_recv()
            if pieces[p][2]:
                along(p, diag + 4 * shift, up, down)

        if k == 0:
            one(0, True, True)
        elif k < nz:
            pl.when(z >= k)(lambda: one(-k, True, False))
            pl.when(z + k < nz)(lambda: one(k, False, True))

    first = core == 0
    state = {}

    def occ_start():
        for d in range(1, n):
            occ_copy(me, (me + d) % n).start()
        occ_dense[...] = jnp.zeros_like(occ_dense)
        vir_dense[...] = jnp.zeros_like(vir_dense)
        x_full[...] = jnp.zeros_like(x_full)

    def half_transform():
        for d in range(1, n):
            occ_copy((me + d) % n, me).wait_recv()
        for w in range(n):
            occ_dense[starts[w]:starts[w] + rows, :] += rows_all[w, :rows, :NOCC]
        l_copy.wait()
        occ_t = occ_dense[...].T[:, :half]
        x_full[:, :nao] = product(split(occ_t), split(l_buf[...]))
        whole = x_full[...]
        low = whole[:, :x_out.shape[1]]
        high = pltpu.roll(whole, x_full.shape[1] - half, 1)[:, :x_out.shape[1]]
        x_out[...] = jnp.where(first, high, low)
        state["own"] = jnp.where(first, low, high)
        pair_copy(0, x_out, x_in).start()

    def x_join():
        pair_copy(0, x_out, x_in).wait_recv()
        x_send[...] = (state["own"] + x_in[...]).reshape(x_send.shape)

    def x_start():
        for d in range(1, n):
            x_copy(me, (me + d) % n).start()
        x_recv[me] = x_send[me]

    def x_wait():
        for d in range(1, n):
            x_copy((me + d) % n, me).wait_recv()

    def join(w):
        vir_dense[starts[w]:starts[w] + rows, :] += rows_all[w, :rows, NOCC:]

    steps = dict(
        occ=occ_start, own=send_own, line=line, plane=plane, corner=corner,
        half=half_transform, xjoin=x_join, xstart=x_start, xwait=x_wait)
    for step, *args in plan:
        steps[step](*args)

    for w in range(n):
        join(w)
    y_full[...] = product(split(x_recv[...].reshape(x_out.shape)), split(vir_dense[...]))
    whole_y = y_full[...]
    low_y = whole_y[:, :y_out.shape[1]]
    high_y = pltpu.roll(whole_y, y_full.shape[1] - out_ref.shape[2], 1)[:, :y_out.shape[1]]
    y_out[...] = jnp.where(first, high_y, low_y)
    y_own = jnp.where(first, low_y, high_y)
    pair_copy(1, y_out, y_in).start()

    for d in range(1, n):
        occ_copy(me, (me + d) % n).wait_send()
        x_copy(me, (me + d) % n).wait_send()
    for p in range(len(pieces)):
        for zz in range(nz):
            w, wd = x + 2 * y + 4 * zz, diag + 4 * (zz - z)
            vir_copy(p, w, 0, xp).wait_send()
            vir_copy(p, w, 1, yp).wait_send()
            for slot in (w, wd) if pieces[p][2] else (w,):
                pl.when((z >= zz) & (z < nz - 1))(lambda: vir_copy(p, slot, 2, xp).wait_send())
                pl.when((z <= zz) & (z > 0))(lambda: vir_copy(p, slot, 3, xp).wait_send())
            crossed = (z == zz) if pieces[p][2] else (z >= 0)
            if zz % 2 == 0:
                pl.when(crossed)(lambda: vir_copy(p, xp + 4 * (zz - z), 1, yp).wait_send())
            else:
                pl.when(crossed)(lambda: vir_copy(p, yp + 4 * (zz - z), 0, xp).wait_send())
    pair_copy(0, x_out, x_in).wait_send()
    pair_copy(1, y_out, y_in).wait()
    out_ref[...] = (y_own + y_in[...])[:, :out_ref.shape[2]].reshape(out_ref.shape)


def plan_of(count, nz):
    every = range(count)
    plan = [("occ",)]
    plan += [("own", p) for p in every]
    plan += [("line", 1, p) for p in every]
    plan += [("half",)]
    plan += [("plane", 0, p) for p in every]
    plan += [("line", 2, p) for p in every]
    plan += [("xjoin",)]
    plan += [("plane", 1, p) for p in every]
    plan += [("xstart",)]
    plan += [("corner", 0, p) for p in every]
    for k in range(2, nz):
        plan += [("line", k + 1, p) for p in every]
        plan += [("plane", k, p) for p in every]
        plan += [("corner", k - 1, p) for p in every]
    plan += [("corner", nz - 1, p) for p in every]
    return plan + [("xwait",)]


def body(n, cholesky, coefficients):
    if cholesky.shape[0] != 1:
        return simple_body(cholesky, coefficients)
    half, nao = cholesky.shape[1:]
    per = coefficients.shape[1]
    nmo = per * n // half
    nvir = nmo - NOCC
    offsets = [w * per % nmo for w in range(n)]
    starts = tuple(w * per // nmo for w in range(n))
    rows = max(-(-(offset + per) // nmo) for offset in offsets)
    deep = up_to(rows, 8)
    me = lax.axis_index("vec")
    flat = coefficients[0]
    total = deep * nmo
    framed = jnp.zeros((total,), F32)
    for offset in sorted(set(offsets)):
        here = jnp.pad(flat, (offset, total - per - offset))
        framed = jnp.where(me * per % nmo == offset, here, framed)
    framed = framed.reshape(deep, nmo)
    wide = up_to(nvir, LANES)
    pieces = tuple((row, min(STEP, deep - row), row < TURN) for row in range(0, deep, STEP))
    plan = plan_of(len(pieces), n // 4)
    tall = up_to(max(half, starts[-1] + rows), LANES)
    part = up_to(nvir // 2, LANES)
    iblock = NOCC // n
    dma = pltpu.SemaphoreType.DMA
    vmem = pl.BlockSpec(memory_space=pltpu.VMEM)
    return pl.pallas_call(
        functools.partial(kernel, n, starts, rows, pieces, plan),
        out_shape=jax.ShapeDtypeStruct((n, iblock, nvir // 2), F32),
        in_specs=[vmem, pl.BlockSpec(memory_space=pl.ANY)],
        out_specs=vmem,
        scratch_shapes=[
            pltpu.VMEM((n, deep, NOCC + wide), F32),
            pltpu.VMEM((half, nao), F32),
            pltpu.VMEM((tall, NOCC), F32),
            pltpu.VMEM((tall, wide), F32),
            pltpu.VMEM((NOCC, up_to(nao, LANES)), F32),
            pltpu.VMEM((NOCC, tall), F32),
            pltpu.VMEM((NOCC, tall), F32),
            pltpu.VMEM((n, iblock, tall), F32),
            pltpu.VMEM((n, iblock, tall), F32),
            pltpu.VMEM((NOCC, wide), F32),
            pltpu.VMEM((NOCC, part), F32),
            pltpu.VMEM((NOCC, part), F32),
            dma, dma((n,)), dma((n,)), dma((len(pieces), 4, n)), dma((len(pieces), n)), dma((n,)), dma((n,)), dma((2,)), dma((2,)),
        ],
        compiler_params=pltpu.CompilerParams(
            collective_id=0, has_side_effects=True, vmem_limit_bytes=60 * 1024 * 1024),
        name="transform",
    )(framed, cholesky[0])


def solution(mesh):
    n = mesh.shape["vec"]
    in_specs = (P("vec", "ao", None), P("ao", "vec"))
    out_specs = P(None, "vec", "ao")
    lines = n % 4 == 0 and mesh.shape["ao"] == 2 and NOCC % (8 * n) == 0
    step = functools.partial(body, n) if lines else simple_body
    return jax.shard_map(step, mesh=mesh, in_specs=in_specs, out_specs=out_specs, check_vma=False)
```

time: 56.7 us -> 52 us (0.917)
  Pallas kernels: 52.2 us -> 48.1 us
  local copies, waits for them, and re-layouts: 3.2 us -> 2.57 us
    pallas_call x1, Pallas kernels: 52.2 us -> 48.1 us  [body(): pl.pallas_call(functools.partial(kernel, n, starts, rows, pieces, plan),...]
    reshape x1, local copies, waits for them, and re-layouts: 0.16 us -> 0.85 us  [body(): framed = framed.reshape(deep, nmo)]
    pad x1 -> x0, local copies, waits for them, and re-layouts: 0.69 us -> none  [body(): vir = jnp.pad(framed[:, NOCC:], ((0, 0), (0, wide - nvir)))]
    slice x2 -> x0, local copies, waits for them, and re-layouts: 0.63 us -> none  [the longest x1 0.61 us: body(): occ = framed[:, :NOCC]]
where the time goes in v2:
time: 52 us; the launch traced here: 51.8 us
  Pallas kernels  48.1 us (92%)
  local copies, waits for them, and re-layouts  2.57 us (5%)
  other arithmetic  1.12 us (2%)
    pallas_call x1, Pallas kernels, body(): pl.pallas_call(functools.partial(kernel, n, starts, rows, pieces, plan),...  48.1 us
    unnamed x1, local copies, waits for them, and re-layouts  1.72 us
    select_n x1, other arithmetic, body(): framed = jnp.where(me * per % nmo == offset, here, framed)  1.12 us

profile of v2, /device:TPU:0, one launch (start us, length us, event | category | flops | bytes accessed | tf_op | source)
XLA Modules:
  0.0 51.8 jit_solution(8074783026202973398)
XLA Ops:
  0.0 1.1 %select_select_fusion = f32[48000]{0:T(1024)S(1)} fusion(f32[45000]{0:T(1024)} %bitcast.3, pred[]{:T(512)S(6)} %eq.10, pred[]{:T(512)S(6)} %eq.9), kind=kLoop, calls=%fused_computation | loop fusion | flops 96000 | bytes 372002 | tf_op jit(solution)/shard_map/jit(_where)/select_n | solution.py:270
  1.1 0.9 %reshape.3.own_ref = f32[40,1200]{1,0:T(8,128)} reshape(f32[48000]{0:T(1024)S(1)} %select_select_fusion) | data formatting | bytes 384000 | tf_op jit(solution)/shard_map/reshape | solution.py:271
  2.0 48.1 %transform.1 = f32[16,8,536]{2,1,0:T(8,128)} custom-call(f32[40,1200]{1,0:T(8,128)} %reshape.3.own_ref, f32[600,1200]{1,0:T(8,128)} %bitcast.2), custom_call_target="tpu_custom_call" | custom-call | tf_op jit(solution)/shard_map/transform/pallas_call | solution.py:280
  50.1 1.7 %copy.4 = f32[16,8,536]{2,1,0:T(8,128)} copy(f32[16,8,536]{2,1,0:T(8,128)} %transform.1) | data formatting | bytes 548864

commit v3 on v2

--- a/solution.py
+++ b/solution.py
@@ -11,7 +11,7 @@
 LANES = 128
 MESH = pl.DeviceIdType.MESH
 F32 = jnp.float32
-STEP, TURN = 16, 0
+STEP, TURN = 24, 0
 
 
 def up_to(size, step):
@@ -77,10 +77,10 @@
     pl.semaphore_signal(barrier, inc=1, device_id=(me, 1 - core), device_id_type=MESH)
     pl.semaphore_wait(barrier, n)
 
-    def occ_copy(w, to):
+    def occ_copy(w, way, to):
         part = rows_all.at[w, :, pl.ds(0, NOCC)]
         return pltpu.make_async_remote_copy(
-            src_ref=part, dst_ref=part, send_sem=occ_ss.at[to], recv_sem=occ_rs.at[w],
+            src_ref=part, dst_ref=part, send_sem=occ_ss.at[way, to if way == 3 else w], recv_sem=occ_rs.at[w],
             device_id=(to, core), device_id_type=MESH)
 
     def vir_copy(p, w, way, to):
@@ -155,16 +155,28 @@
     first = core == 0
     state = {}
 
+    def occ_spread(w):
+        for way, to in enumerate((xp, yp, diag)):
+            occ_copy(w, way, to).start()
+
+    def occ_line():
+        for d in range(1, nz):
+            w = (me + 4 * d) % n
+            occ_copy(w, 3, me).wait_recv()
+            occ_spread(w)
+
     def occ_start():
-        for d in range(1, n):
-            occ_copy(me, (me + d) % n).start()
+        for d in range(1, nz):
+            occ_copy(me, 3, (me + 4 * d) % n).start()
+        occ_spread(me)
         occ_dense[...] = jnp.zeros_like(occ_dense)
         vir_dense[...] = jnp.zeros_like(vir_dense)
         x_full[...] = jnp.zeros_like(x_full)
 
     def half_transform():
-        for d in range(1, n):
-            occ_copy((me + d) % n, me).wait_recv()
+        for d in range(nz):
+            for other in (xp, yp, diag):
+                occ_copy((other + 4 * d) % n, 3, me).wait_recv()
         for w in range(n):
             occ_dense[starts[w]:starts[w] + rows, :] += rows_all[w, :rows, :NOCC]
         l_copy.wait()
@@ -194,7 +206,7 @@
         vir_dense[starts[w]:starts[w] + rows, :] += rows_all[w, :rows, NOCC:]
 
     steps = dict(
-        occ=occ_start, own=send_own, line=line, plane=plane, corner=corner,
+        occ=occ_start, occline=occ_line, own=send_own, line=line, plane=plane, corner=corner,
         half=half_transform, xjoin=x_join, xstart=x_start, xwait=x_wait)
     for step, *args in plan:
         steps[step](*args)
@@ -210,8 +222,12 @@
     pair_copy(1, y_out, y_in).start()
 
     for d in range(1, n):
-        occ_copy(me, (me + d) % n).wait_send()
         x_copy(me, (me + d) % n).wait_send()
+    for d in range(nz):
+        for way in range(3):
+            occ_copy((me + 4 * d) % n, way, xp).wait_send()
+        if d:
+            occ_copy(me, 3, (me + 4 * d) % n).wait_send()
     for p in range(len(pieces)):
         for zz in range(nz):
             w, wd = x + 2 * y + 4 * zz, diag + 4 * (zz - z)
@@ -232,22 +248,16 @@
 
 def plan_of(count, nz):
     every = range(count)
-    plan = [("occ",)]
-    plan += [("own", p) for p in every]
-    plan += [("line", 1, p) for p in every]
-    plan += [("half",)]
-    plan += [("plane", 0, p) for p in every]
-    plan += [("line", 2, p) for p in every]
-    plan += [("xjoin",)]
-    plan += [("plane", 1, p) for p in every]
-    plan += [("xstart",)]
-    plan += [("corner", 0, p) for p in every]
-    for k in range(2, nz):
-        plan += [("line", k + 1, p) for p in every]
-        plan += [("plane", k, p) for p in every]
-        plan += [("corner", k - 1, p) for p in every]
-    plan += [("corner", nz - 1, p) for p in every]
-    return plan + [("xwait",)]
+
+    def wave(name, k):
+        return [(name, k, p) for p in every]
+
+    plan = [("occ",), ("own", 0), ("occline",)] + [("own", p) for p in every[1:]]
+    plan += wave("line", 1) + wave("plane", 0) + wave("line", 2) + [("half",)] + wave("plane", 1) + [("xjoin",)] + wave("line", 3) + [("xstart",)] + wave("corner", 0)
+    plan += wave("plane", 2) + wave("corner", 1)
+    for k in range(3, nz):
+        plan += wave("line", k + 1) + wave("plane", k) + wave("corner", k - 1)
+    return plan + wave("corner", nz - 1) + [("xwait",)]
 
 
 def body(n, cholesky, coefficients):
@@ -295,7 +305,7 @@
             pltpu.VMEM((NOCC, wide), F32),
             pltpu.VMEM((NOCC, part), F32),
             pltpu.VMEM((NOCC, part), F32),
-            dma, dma((n,)), dma((n,)), dma((len(pieces), 4, n)), dma((len(pieces), n)), dma((n,)), dma((n,)), dma((2,)), dma((2,)),
+            dma, dma((4, n)), dma((n,)), dma((len(pieces), 4, n)), dma((len(pieces), n)), dma((n,)), dma((n,)), dma((2,)), dma((2,)),
         ],
         compiler_params=pltpu.CompilerParams(
             collective_id=0, has_side_effects=True, vmem_limit_bytes=60 * 1024 * 1024),

time: 52 us -> 49.7 us (0.956)
  Pallas kernels: 48.1 us -> 45.8 us
    pallas_call x1, Pallas kernels: 48.1 us -> 45.8 us  [body(): pl.pallas_call(functools.partial(kernel, n, starts, rows, pieces, plan),...]
where the time goes in v3:
time: 49.7 us; the launch traced here: 49.5 us
  Pallas kernels  45.8 us (92%)
  local copies, waits for them, and re-layouts  2.57 us (5%)
  other arithmetic  1.12 us (2%)
    pallas_call x1, Pallas kernels, body(): pl.pallas_call(functools.partial(kernel, n, starts, rows, pieces, plan),...  45.8 us
    unnamed x1, local copies, waits for them, and re-layouts  1.72 us
    select_n x1, other arithmetic, body(): framed = jnp.where(me * per % nmo == offset, here, framed)  1.12 us

profile of v3, /device:TPU:0, one launch (start us, length us, event | category | flops | bytes accessed | tf_op | source)
XLA Modules:
  0.0 49.5 jit_solution(12427932316232675722)
XLA Ops:
  0.0 1.1 %select_select_fusion = f32[48000]{0:T(1024)S(1)} fusion(f32[45000]{0:T(1024)} %bitcast.3, pred[]{:T(512)S(6)} %eq.10, pred[]{:T(512)S(6)} %eq.9), kind=kLoop, calls=%fused_computation | loop fusion | flops 96000 | bytes 372002 | tf_op jit(solution)/shard_map/jit(_where)/select_n | solution.py:280
  1.1 0.9 %reshape.3.own_ref = f32[40,1200]{1,0:T(8,128)} reshape(f32[48000]{0:T(1024)S(1)} %select_select_fusion) | data formatting | bytes 384000 | tf_op jit(solution)/shard_map/reshape | solution.py:281
  2.0 45.8 %transform.1 = f32[16,8,536]{2,1,0:T(8,128)} custom-call(f32[40,1200]{1,0:T(8,128)} %reshape.3.own_ref, f32[600,1200]{1,0:T(8,128)} %bitcast.2), custom_call_target="tpu_custom_call" | custom-call | tf_op jit(solution)/shard_map/transform/pallas_call | solution.py:290
  47.8 1.7 %copy.4 = f32[16,8,536]{2,1,0:T(8,128)} copy(f32[16,8,536]{2,1,0:T(8,128)} %transform.1) | data formatting | bytes 548864
